TPU v7x, 32 devices: a whole 2x2x4 slice. The times are simulated.
32 devices in a mesh: groups: 2 (over y), seq: 4 (over z), heads: 2 (over x), cfg: 2 (over core).
Axes of the slice: x: 2, y: 2, z: 4, core: 2. Of those that a mesh axis runs over, the one named last changes fastest.
Arguments:
- video_tokens: bfloat16 [2, 8, 1152, 1024], P('cfg', ('groups', 'seq'), 'heads'), parts along dimension 1, may hold values from -6 to 6
- text_tokens: bfloat16 [2, 8, 1152, 128], P('cfg', ('groups', 'seq'), 'heads'), parts along dimension 1, may hold values from -6 to 6
- text_length: int32 [2, 8], P('cfg', ('groups', 'seq')), parts along dimension 1, may hold values from 1 to 128
- guide_numer: int32 [8], P(('groups', 'seq')), parts along dimension 0, may hold values from 2 to 8
- guide_denom: int32 [8], P(('groups', 'seq')), parts along dimension 0, may hold values from 4 to 8
- spatial_gain: bfloat16 [1152], replicated, may hold values from 0.25 to 1.75
- spatial_qkv: bfloat16 [3, 1152, 1152], P(None, 'heads'), may hold values from -0.11785113 to 0.11785113
- spatial_out: bfloat16 [1152, 1152], P('heads'), may hold values from -0.1875 to 0.1875
- temporal_gain: bfloat16 [1152], replicated, may hold values from 0.25 to 1.75
- temporal_qkv: bfloat16 [3, 1152, 1152], P(None, 'heads'), may hold values from -0.11785113 to 0.11785113
- temporal_out: bfloat16 [1152, 1152], P('heads'), may hold values from -0.1875 to 0.1875
Outputs:
- guided: bfloat16 [8, 1152, 1024], P(('groups', 'seq'), ('heads', 'cfg')), parts along dimension 0
There are 2 independent parts, one for each index of `groups`. A program takes and returns all parts, laid end to end along the dimension named above; an argument that names none is the same for every part. Nothing has to cross between parts.
Inputs may be any that keep to these rules, and one draw needn't show every extreme that they name: `text_length`: text tokens at or beyond a frame's length are padding.
All inputs are finite; a program needn't handle non-finite values.
Results may differ from a plain program's by a relative error of at most 0.009.
Values may be sent and summed in bfloat16 or wider, within the bound.
A program may use at most 64 MiB of HBM per device.

v0:
```python
import jax
import jax.numpy as jnp
from jax import lax
from jax.sharding import PartitionSpec as P

D = 1152
HEAD_DIM = 72
epsilon = 1e-06


def from_partner(shard, axis, stride):
    return lax.ppermute(shard, axis, [(i, i ^ 1 << stride) for i in range(lax.axis_size(axis))])


def softmax_along(scores, axis):
    top_score = jnp.max(scores, axis=axis, keepdims=True)
    expons = jnp.exp(scores - top_score)
    return (expons / jnp.sum(expons, axis=axis, keepdims=True)).astype(jnp.bfloat16)


def project_piece(piece, gain_vector, weights, parts):
    gain_piece = gain_vector.astype(jnp.float32)
    weight_piece = weights[parts]
    piece_wide = piece.astype(jnp.float32)
    scaled = (piece_wide * gain_piece[None, :, None]).astype(jnp.bfloat16)
    product = jnp.einsum("kod,fdp->fkop", weight_piece, scaled, preferred_element_type=jnp.float32)
    return (product, jnp.sum(piece_wide * piece_wide, axis=1))


def add_mixed(piece, matrix):
    return jnp.einsum("oc,fcp->fop", matrix, piece, preferred_element_type=jnp.float32)


def shards(
    video_tokens,
    text_tokens,
    text_length,
    guide_numer,
    guide_denom,
    spatial_gain,
    spatial_qkv,
    spatial_out,
    temporal_gain,
    temporal_qkv,
    temporal_out,
):
    frame_count = video_tokens.shape[1]
    width = video_tokens.shape[2]
    positions = video_tokens.shape[3]
    text_count = text_tokens.shape[3]
    local_heads = width // HEAD_DIM
    frame_tokens = video_tokens[0]
    frame_text = text_tokens[0]
    video_piece = lax.all_gather(frame_tokens, "heads", axis=1, tiled=True)
    text_piece = lax.all_gather(frame_text, "heads", axis=1, tiled=True)
    video_add, video_sq = project_piece(video_piece, spatial_gain, spatial_qkv, slice(0, 3))
    text_add, text_sq = project_piece(text_piece, spatial_gain, spatial_qkv, slice(1, 3))
    mixed = (video_add * lax.rsqrt(video_sq / D + epsilon)[:, None, None, :]).astype(jnp.bfloat16)
    mixed = mixed.reshape(frame_count, 3, local_heads, HEAD_DIM, positions)
    context = (text_add * lax.rsqrt(text_sq / D + epsilon)[:, None, None, :]).astype(jnp.bfloat16)
    context = context.reshape(frame_count, 2, local_heads, HEAD_DIM, text_count)
    key_rows = jnp.concatenate([mixed[:, 1], context[:, 0]], axis=3)
    value_rows = jnp.concatenate([mixed[:, 2], context[:, 1]], axis=3)
    query_all = mixed[:, 0]
    text_valid = jnp.arange(text_count, dtype=jnp.int32)[None, :] < text_length[0][:, None]
    valid_keys = jnp.concatenate(
        [jnp.ones((frame_count, positions), dtype=bool), text_valid], axis=1
    )
    block_rows = min(512, positions)
    block_count = positions // block_rows
    frame_ids = jnp.repeat(jnp.arange(frame_count, dtype=jnp.int32), block_count)
    block_ids = jnp.tile(jnp.arange(block_count, dtype=jnp.int32), frame_count)

    def block_step(inputs):
        frame_id, block_id = inputs
        query_rows = lax.dynamic_slice_in_dim(
            query_all[frame_id], block_id * block_rows, block_rows, 2
        )
        scores = jnp.einsum(
            "hep,hek->hpk", query_rows, key_rows[frame_id], preferred_element_type=jnp.float32
        )
        scores = scores * HEAD_DIM ** (-0.5)
        scores = jnp.where(valid_keys[frame_id][None, None, :], scores, -jnp.inf)
        weights = softmax_along(scores, 2)
        result = jnp.einsum(
            "hpk,hek->hep", weights, value_rows[frame_id], preferred_element_type=jnp.float32
        )
        return result.astype(jnp.bfloat16)

    attended = lax.map(block_step, (frame_ids, block_ids))
    attended = attended.reshape(frame_count, block_count, local_heads, HEAD_DIM, block_rows)
    attended = jnp.transpose(attended, (0, 2, 3, 1, 4)).reshape(frame_count, width, positions)
    update = add_mixed(lax.all_gather(attended, "heads", axis=1, tiled=True), spatial_out)
    after_spatial = (frame_tokens.astype(jnp.float32) + update).astype(jnp.bfloat16)
    own_rows = lax.all_to_all(after_spatial, "seq", split_axis=2, concat_axis=0, tiled=True)
    frames_all = own_rows.shape[0]
    columns = own_rows.shape[2]
    piece_add, piece_sq = project_piece(
        lax.all_gather(own_rows, "heads", axis=1, tiled=True),
        temporal_gain,
        temporal_qkv,
        slice(0, 3),
    )
    mixed_time = (piece_add * lax.rsqrt(piece_sq / D + epsilon)[:, None, None, :]).astype(
        jnp.bfloat16
    )
    mixed_time = mixed_time.reshape(frames_all, 3, local_heads, HEAD_DIM, columns)
    time_scores = jnp.einsum(
        "fhep,ghep->hfgp", mixed_time[:, 0], mixed_time[:, 1], preferred_element_type=jnp.float32
    )
    time_weights = softmax_along(time_scores * HEAD_DIM ** (-0.5), 2)
    attended_time = jnp.einsum(
        "hfgp,ghep->fhep", time_weights, mixed_time[:, 2], preferred_element_type=jnp.float32
    )
    attended_time = attended_time.astype(jnp.bfloat16).reshape(frames_all, width, columns)
    update_time = add_mixed(
        lax.all_gather(attended_time, "heads", axis=1, tiled=True), temporal_out
    )
    block_out = (own_rows.astype(jnp.float32) + update_time).astype(jnp.bfloat16)
    returned = lax.all_to_all(block_out, "seq", split_axis=0, concat_axis=2, tiled=True)
    half_width = width // 2
    partner = from_partner(returned, "cfg", 0)
    branch_index = lax.axis_index("cfg")
    cond_full = jnp.where(branch_index == 0, returned, partner)
    uncond_full = jnp.where(branch_index == 0, partner, returned)
    cond_part = lax.dynamic_slice_in_dim(cond_full, branch_index * half_width, half_width, 1)
    uncond_part = lax.dynamic_slice_in_dim(uncond_full, branch_index * half_width, half_width, 1)
    ratio = guide_numer.astype(jnp.float32) / guide_denom.astype(jnp.float32)
    cond_wide = cond_part.astype(jnp.float32)
    uncond_wide = uncond_part.astype(jnp.float32)
    return (uncond_wide + ratio[:, None, None] * (cond_wide - uncond_wide)).astype(jnp.bfloat16)


def solution(mesh):
    return jax.shard_map(
        shards,
        mesh=mesh,
        in_specs=(
            P("cfg", ("groups", "seq"), "heads", None),
            P("cfg", ("groups", "seq"), "heads", None),
            P("cfg", ("groups", "seq")),
            P(("groups", "seq")),
            P(("groups", "seq")),
            P(),
            P(None, "heads", None),
            P("heads", None),
            P(),
            P(None, "heads", None),
            P("heads", None),
        ),
        out_specs=P(("groups", "seq"), ("heads", "cfg"), None),
        check_vma=False,
    )
```

profile of v0, /device:TPU:0, one launch (start us, length us, event | category | flops | bytes accessed | tf_op | source)
XLA Modules:
  0.0 359.0 jit_solution(843548291912899709)
XLA Ops:
  8.7 7.7 %all-gather.1 = bf16[1,1,1152,128]{3,2,1,0:T(8,128)(2,1)S(1)} all-gather(bf16[1,1,576,128]{3,2,1,0:T(8,128)(2,1)} %param.14), channel_id=3, replica_groups=mesh['groups'=2,'seq'=4,'heads'=2,'cfg'=2] {'heads'}, dimensions={2}, use_global_device_ids=true | all-gather | bytes 442368 | tf_op jit(solution)/shard_map/all_gather | solution.py:55
  16.6 3.0 fusion.87
  19.6 28.1 %all-gather.12.cloned.1.call-done = bf16[1,1,1152,1024]{3,2,1,0:T(8,128)(2,1)} async-done(((bf16[1,1,576,1024]{3,2,1,0:T(8,128)(2,1)}), bf16[1,1,1152,1024]{3,2,1,0:T(8,128)(2,1)}) %all-gather.12.cloned.1.call-update) | async-done | bytes 2359312 | tf_op jit(solution)/shard_map/all_gather | solution.py:54
  50.1 7.3 %fusion.48 = bf16[1,1024,3,576]{1,3,2,0:T(8,128)(2,1)S(1)} fusion(f32[1024]{0:T(1024)S(1)} %add_rsqrt_fusion.1, bf16[3,576,1152]{2,1,0:T(8,128)(2,1)} %param.19, bf16[1,1,1152,1024]{3,2,1,0:T(8,128)(2,1)S(1)} %copy-done.3, f32[1152]{0:T(1024)S(1)} %convert_element_type.98), kind=kOutput, calls=%fused_computation.28 | convolution fusion | flops 4083941376 | bytes 9888256 | tf_op jit(solution)/shard_map/kod,fdp->fkop/dot_general | solution.py:26
  60.1 37.0 %while.10 = (s32[]{:T(128)}, bf16[2,8,72,512]{3,2,1,0:T(8,128)(2,1)}, pred[1,1152]{1,0:T(4,128)(4,1)S(1)}, s32[2]{0:T(128)S(1)}, bf16[1,8,72,1024]{3,2,1,0:T(8,1...) while((s32[]{:T(128)}, ...), condition=%wide.region_5.6_spmd, body=%wide.region_2.5_spmd.sunk | while | flops 2081200384 | bytes 5788856 | solution.py:90
  61.9 7.0 %exponential_reduce_fusion.2 = f32[8,512]{1,0:T(8,128)S(1)} fusion(pred[1152]{0:T(1024)(128)(4,1)S(1)} %reduce.5, bf16[1,8,72,1152]{3,2,1,0:T(8,128)(2,1)S(1)} %get-tuple-element.139, bf16[1,8,72,1024]{3,2,1,0:T(8,128)(2,1)} %get-tuple-element.138, s32[]{:T(128)S(6)} %select_n.52), kind=kOutput, calls=%fused_computation.5.clone.1 | convolution fusion | flops 698352768 | bytes 1934468 | tf_op jit(solution)/shard_map/while/body/eval_jaxpr/sub | solution.py:17
  69.0 9.8 %fusion.120 = bf16[2,8,72,512]{3,2,1,0:T(8,128)(2,1)} fusion(bf16[2,8,72,512]{3,2,1,0:T(8,128)(2,1)} %get-tuple-element.123, s32[]{:T(128)} %get-tuple-element.122, bf16[1,8,72,1152]{3,2,1,0:T(8,128)(2,1)} %get-tuple-element.140, f32[8,512]{1,0:T(8,128)S(1)} %exponential_reduce_fusion.2, pred[1152]{0:T(1024)(128)(4,1)S(1)} %reduce.5, ...), kind=kOutput, calls=%fused_computation.13.clone.1 | convolution fusion | flops 1382847616 | bytes 3851908 | tf_op jit(solution)/shard_map/while/body/eval_jaxpr/hpk,hek->hep/dot_general | solution.py:85
  80.2 7.0 %exponential_reduce_fusion.2 = f32[8,512]{1,0:T(8,128)S(1)} fusion(pred[1152]{0:T(1024)(128)(4,1)S(1)} %reduce.5, bf16[1,8,72,1152]{3,2,1,0:T(8,128)(2,1)S(1)} %get-tuple-element.139, bf16[1,8,72,1024]{3,2,1,0:T(8,128)(2,1)} %get-tuple-element.138, s32[]{:T(128)S(6)} %select_n.52), kind=kOutput, calls=%fused_computation.5.clone.1 | convolution fusion | flops 698352768 | bytes 1934468 | tf_op jit(solution)/shard_map/while/body/eval_jaxpr/sub | solution.py:17
  87.2 9.8 %fusion.120 = bf16[2,8,72,512]{3,2,1,0:T(8,128)(2,1)} fusion(bf16[2,8,72,512]{3,2,1,0:T(8,128)(2,1)} %get-tuple-element.123, s32[]{:T(128)} %get-tuple-element.122, bf16[1,8,72,1152]{3,2,1,0:T(8,128)(2,1)} %get-tuple-element.140, f32[8,512]{1,0:T(8,128)S(1)} %exponential_reduce_fusion.2, pred[1152]{0:T(1024)(128)(4,1)S(1)} %reduce.5, ...), kind=kOutput, calls=%fused_computation.13.clone.1 | convolution fusion | flops 1382847616 | bytes 3851908 | tf_op jit(solution)/shard_map/while/body/eval_jaxpr/hpk,hek->hep/dot_general | solution.py:85
  101.5 36.0 %all-gather.8.cloned.1.call-done = bf16[1,1152,1024]{2,1,0:T(8,128)(2,1)} async-done(((bf16[1,576,1024]{2,1,0:T(8,128)(2,1)}), bf16[1,1152,1024]{2,1,0:T(8,128)(2,1)}) %all-gather.8.cloned.1.call-update) | async-done | bytes 2359312 | tf_op jit(solution)/shard_map/all_gather | solution.py:93
  137.5 3.7 %fusion.64 = bf16[1,576,1024]{2,1,0:T(8,128)(2,1)S(1)} fusion(bf16[576,1152]{1,0:T(8,128)(2,1)S(1)} %copy-done, bf16[1,1152,1024]{2,1,0:T(8,128)(2,1)} %all-gather.8.cloned.1.call-done, bf16[1,1,576,1024]{3,2,1,0:T(8,128)(2,1)} %param.13), kind=kOutput, calls=%fused_computation.47 | convolution fusion | flops 1360723968 | bytes 6045696 | tf_op jit(solution)/shard_map/oc,fcp->fop/dot_general | solution.py:31
  141.1 4.1 %copy.44 = bf16[1,576,1024]{1,0,2:T(2,128)(2,1)} copy(bf16[1,576,1024]{2,1,0:T(8,128)(2,1)S(1)} %fusion.64) | data formatting | bytes 2359296 | tf_op jit(solution)/shard_map/convert_element_type | solution.py:94
  145.8 9.9 %reduce.3 = bf16[1024,576]{1,0:T(8,128)(2,1)S(1)} reduce(bf16[1024,1,576]{2,1,0:T(2,128)(2,1)} %bitcast.189, bf16[]{:T(256)} %broadcast.82), dimensions={1}, to_apply=%bitcast.164.reduce_sub_computation | reduce | bytes 2359298
  158.3 33.0 %all_to_all.36 = bf16[4,2,73728]{2,1,0:T(2,128)(2,1)S(1)} all-to-all(bf16[4,2,73728]{2,1,0:T(2,128)(2,1)} %reshape.124), channel_id=1, replica_groups=mesh['groups'=2,'seq'=4,'heads'=2,'cfg'=2] {'seq'}, dimensions={0} | all-to-all | bytes 2359296 | tf_op jit(solution)/shard_map/all_to_all | solution.py:95
  191.3 3.3 reshape.125
  198.3 34.1 %all-gather.14.cloned.1.call-done = bf16[4,1,1152,256]{3,2,0,1:T(8,128)(2,1)} async-done(((bf16[4,1,576,256]{3,2,0,1:T(8,128)(2,1)}), bf16[4,1,1152,256]{3,2,0,1:T(8,128)(2,1)}) %all-gather.14.cloned.1.call-update) | async-done | bytes 2359312 | tf_op jit(solution)/shard_map/all_gather | solution.py:99
  234.7 7.2 %multiply_convert_fusion = bf16[4,256,3,576]{1,3,2,0:T(8,128)(2,1)S(1)} fusion(f32[4,256]{1,0:T(4,128)S(1)} %add_rsqrt_fusion, bf16[3,576,1152]{2,1,0:T(8,128)(2,1)} %param.22, bf16[4,1,1152,256]{3,2,0,1:T(8,128)(2,1)S(1)} %copy-done.4, f32[1152]{0:T(1024)S(1)} %convert_element_type.109), kind=kOutput, calls=%fused_computation.29 | convolution fusion | flops 4083941376 | bytes 9888256 | tf_op jit(solution)/shard_map/kod,fdp->fkop/dot_general | solution.py:26
  246.7 4.1 %copy.60 = bf16[4,1,8,72,256]{3,0,4,2,1:T(4,128)(2,1)} copy(bf16[4,1,8,72,256]{4,3,2,1,0:T(8,128)(2,1)} %get-tuple-element.59) | data formatting | bytes 2359296
  250.7 5.8 %fusion.71 = f32[8,256,4,4]{3,2,1,0:T(4,128)} fusion(bf16[4,1,8,72,256]{3,0,4,2,1:T(4,128)(2,1)} %copy.60, bf16[4,1,8,72,256]{3,0,4,2,1:T(4,128)(2,1)S(1)} %copy.59), kind=kOutput, calls=%fused_computation.54 | convolution fusion | flops 4718592 | bytes 2490368 | tf_op jit(solution)/shard_map/fhep,ghep->hfgp/dot_general | solution.py:108
  264.1 5.8 %convert_bitcast_fusion = bf16[4,8,72,256]{2,0,3,1:T(4,128)(2,1)} fusion(bf16[8,4,4,256]{2,1,3,0:T(4,128)(2,1)} %copy.51, bf16[4,1,8,72,256]{3,0,4,2,1:T(4,128)(2,1)} %copy.58), kind=kOutput, calls=%fused_computation.59 | convolution fusion | flops 5308416 | bytes 2424832 | tf_op jit(solution)/shard_map/hfgp,ghep->fhep/dot_general | solution.py:112
  269.9 4.2 %copy.52 = bf16[4,8,72,256]{3,2,1,0:T(8,128)(2,1)} copy(bf16[4,8,72,256]{2,0,3,1:T(4,128)(2,1)} %convert_bitcast_fusion) | data formatting | bytes 2359296 | tf_op jit(solution)/shard_map/convert_element_type | solution.py:115
  274.1 36.2 %all-gather.10.cloned.1.call-done = bf16[4,1152,256]{2,1,0:T(8,128)(2,1)} async-done(((bf16[4,576,256]{2,1,0:T(8,128)(2,1)}), bf16[4,1152,256]{2,1,0:T(8,128)(2,1)}) %all-gather.10.cloned.1.call-update) | async-done | bytes 2359312 | tf_op jit(solution)/shard_map/all_gather | solution.py:117
  310.3 3.8 %fusion.63 = bf16[4,576,256]{2,1,0:T(8,128)(2,1)S(1)} fusion(bf16[4,1152,256]{2,1,0:T(8,128)(2,1)} %all-gather.10.cloned.1.call-done, bf16[576,1152]{1,0:T(8,128)(2,1)} %param.23, bf16[1,576,4,256]{3,1,2,0:T(8,128)(2,1)S(1)} %copy-done.2), kind=kOutput, calls=%fused_computation.45 | convolution fusion | flops 1360723968 | bytes 6045696 | tf_op jit(solution)/shard_map/oc,fcp->fop/dot_general | solution.py:31
  314.1 32.8 %all_to_all.37 = bf16[4,576,256]{2,1,0:T(8,128)(2,1)S(1)} all-to-all(bf16[4,576,256]{2,1,0:T(8,128)(2,1)S(1)} %fusion.63), channel_id=1, replica_groups=mesh['groups'=2,'seq'=4,'heads'=2,'cfg'=2] {'seq'}, dimensions={0} | all-to-all | bytes 2359296 | tf_op jit(solution)/shard_map/all_to_all | solution.py:120
  (57 shorter events, 38.0 us)
Async XLA Ops:
  6.5 130.9 %copy-start = (bf16[576,1152]{1,0:T(8,128)(2,1)S(1)}, bf16[576,1152]{1,0:T(8,128)(2,1)}, u32[]{:S(2)}) copy-start(bf16[576,1152]{1,0:T(8,128)(2,1)} %param.20) | copy-start | bytes 3981316
  6.5 41.1 %all-gather.12.cloned.1.call-start = ((), (), s32[]{:S(2)}) async-start(), calls=%async_computation.4 | async-start | bytes 3538944 | tf_op jit(solution)/shard_map/all_gather | solution.py:54
  7.3 130.2 %all-gather.8.cloned.1.call-start = ((), (), s32[]{:S(2)}) async-start(), calls=%async_computation.2 | async-start | bytes 3538944 | tf_op jit(solution)/shard_map/all_gather | solution.py:93
  47.7 2.4 copy-start.3
  101.3 131.0 %all-gather.14.cloned.1.call-start = ((), (), s32[]{:S(2)}) async-start(), calls=%async_computation.5 | async-start | bytes 3538944 | tf_op jit(solution)/shard_map/all_gather | solution.py:99
  196.5 1.8 copy-start.5
  198.0 112.3 %all-gather.10.cloned.1.call-start = ((), (), s32[]{:S(2)}) async-start(), calls=%async_computation.3 | async-start | bytes 3538944 | tf_op jit(solution)/shard_map/all_gather | solution.py:117
  232.3 2.4 copy-start.4
  259.4 2.2 copy-start.1
  269.9 40.4 %copy-start.2 = (bf16[1,576,4,256]{3,1,2,0:T(8,128)(2,1)S(1)}, bf16[1,576,4,256]{3,1,2,0:T(8,128)(2,1)}, u32[]{:S(2)}) copy-start(bf16[1,576,4,256]{3,1,2,0:T(8,128)(2,1)} %copy.46) | copy-start | bytes 3538948
  347.0 3.0 collective-permute-start
Sparse Core Ops, SparseCore 0:
  8.9 38.7 all-gather.11
  101.4 36.0 all-gather.7
  198.1 34.1 all-gather.13
  274.2 36.0 all-gather.9
where the time goes:
time: 364 us; the launch traced here: 359 us
  waiting for transfers between devices  137 us (38%)
  blocking collectives  73.5 us (20%)
  matrix products  70.3 us (19%)
  local copies, waits for them, and re-layouts  41.4 us (11%)
  other arithmetic  19.1 us (5%)
  between operations  15.5 us (4%)
    all_gather x1, waiting for transfers between devices, shards(): lax.all_gather(attended_time, 'heads', axis=1, tiled=True)  36.2 us
    all_gather x1, waiting for transfers between devices, shards(): lax.all_gather(attended, 'heads', axis=1, tiled=True)  36 us
    all_gather x1, waiting for transfers between devices, shards(): lax.all_gather(own_rows, 'heads', axis=1, tiled=True)  34.1 us
    all_to_all x1, blocking collectives, shards(): lax.all_to_all(after_spatial, 'seq', split_axis=2, concat_axis=0, tiled=T...  33 us
    all_to_all x1, blocking collectives, shards(): lax.all_to_all(block_out, 'seq', split_axis=0, concat_axis=2, tiled=True)  32.8 us
    all_gather x1, waiting for transfers between devices, shards(): video_piece = lax.all_gather(frame_tokens, 'heads', axis=1, tiled=True)  28.1 us
    dot_general x2, matrix products, block_step(): jnp.einsum('hpk,hek->hep', weights, value_rows[frame_id], preferred_eleme...  19.7 us
    unnamed x19, local copies, waits for them, and re-layouts  17.8 us
  transfers between devices with their start and end apart: 5, of which 5 were waited for; matrix products, arithmetic and copies ran while one was open for 1% of the time, Pallas kernels for 0%

commit v1 on v0

--- a/solution.py
+++ b/solution.py
@@ -6,6 +6,13 @@
 D = 1152
 HEAD_DIM = 72
 epsilon = 1e-06
+
+
+def with_the_other(array, axis, d):
+    swap = [(0, 1), (1, 0)]
+    both = jnp.concatenate([array, lax.ppermute(array, axis, swap)], axis=d)
+    places = lax.axis_index(axis) * array.shape[d]
+    return jnp.roll(both, places, axis=d)
 
 
 def from_partner(shard, axis, stride):
@@ -113,9 +120,7 @@
         "hfgp,ghep->fhep", time_weights, mixed_time[:, 2], preferred_element_type=jnp.float32
     )
     attended_time = attended_time.astype(jnp.bfloat16).reshape(frames_all, width, columns)
-    update_time = add_mixed(
-        lax.all_gather(attended_time, "heads", axis=1, tiled=True), temporal_out
-    )
+    update_time = add_mixed(with_the_other(attended_time, "heads", 1), temporal_out)
     block_out = (own_rows.astype(jnp.float32) + update_time).astype(jnp.bfloat16)
     returned = lax.all_to_all(block_out, "seq", split_axis=0, concat_axis=2, tiled=True)
     half_width = width // 2

time: 364 us -> 357 us (0.981)
  waiting for transfers between devices: 137 us -> 128 us
    all_gather x1 -> x0, waiting for transfers between devices: 36.2 us -> none  [shards(): lax.all_gather(attended_time, 'heads', axis=1, tiled=True)]
    ppermute x0 -> x1, waiting for transfers between devices: none -> 27.5 us  [with_the_other(): both = jnp.concatenate([array, lax.ppermute(array, axis, swap)], axis=d)]
where the time goes in v1:
time: 357 us; the launch traced here: 352 us
  waiting for transfers between devices  128 us (36%)
  blocking collectives  72.8 us (20%)
  matrix products  72.3 us (20%)
  local copies, waits for them, and re-layouts  41.6 us (12%)
  other arithmetic  19.1 us (5%)
  between operations  15.6 us (4%)
    all_gather x1, waiting for transfers between devices, shards(): lax.all_gather(attended, 'heads', axis=1, tiled=True)  36 us
    all_gather x1, waiting for transfers between devices, shards(): lax.all_gather(own_rows, 'heads', axis=1, tiled=True)  34.3 us
    all_to_all x1, blocking collectives, shards(): lax.all_to_all(after_spatial, 'seq', split_axis=2, concat_axis=0, tiled=T...  33.2 us
    all_to_all x1, blocking collectives, shards(): lax.all_to_all(block_out, 'seq', split_axis=0, concat_axis=2, tiled=True)  31.9 us
    all_gather x1, waiting for transfers between devices, shards(): video_piece = lax.all_gather(frame_tokens, 'heads', axis=1, tiled=True)  28.1 us
    ppermute x1, waiting for transfers between devices, with_the_other(): both = jnp.concatenate([array, lax.ppermute(array, axis, swap)], axis=d)  27.5 us
    dot_general x2, matrix products, block_step(): jnp.einsum('hpk,hek->hep', weights, value_rows[frame_id], preferred_eleme...  19.7 us
    unnamed x19, local copies, waits for them, and re-layouts  17.8 us
  transfers between devices with their start and end apart: 5, of which 5 were waited for; matrix products, arithmetic and copies ran while one was open for 1% of the time, Pallas kernels for 0%

profile of v1, /device:TPU:0, one launch (start us, length us, event | category | flops | bytes accessed | tf_op | source)
XLA Modules:
  0.0 352.3 jit_solution(991237083070920224)
XLA Ops:
  8.7 7.7 %all-gather.1 = bf16[1,1,1152,128]{3,2,1,0:T(8,128)(2,1)S(1)} all-gather(bf16[1,1,576,128]{3,2,1,0:T(8,128)(2,1)} %param.14), channel_id=3, replica_groups=mesh['groups'=2,'seq'=4,'heads'=2,'cfg'=2] {'heads'}, dimensions={2}, use_global_device_ids=true | all-gather | bytes 442368 | tf_op jit(solution)/shard_map/all_gather | solution.py:62
  16.6 3.0 fusion.94
  19.6 28.1 %all-gather.9.cloned.1.call-done = bf16[1,1,1152,1024]{3,2,1,0:T(8,128)(2,1)} async-done(((bf16[1,1,576,1024]{3,2,1,0:T(8,128)(2,1)}), bf16[1,1,1152,1024]{3,2,1,0:T(8,128)(2,1)}) %all-gather.9.cloned.1.call-update) | async-done | bytes 2359312 | tf_op jit(solution)/shard_map/all_gather | solution.py:61
  50.1 7.3 %fusion.48 = bf16[1,1024,3,576]{1,3,2,0:T(8,128)(2,1)S(1)} fusion(f32[1024]{0:T(1024)S(1)} %add_rsqrt_fusion.1, bf16[3,576,1152]{2,1,0:T(8,128)(2,1)} %param.19, bf16[1,1,1152,1024]{3,2,1,0:T(8,128)(2,1)S(1)} %copy-done.3, f32[1152]{0:T(1024)S(1)} %convert_element_type.98), kind=kOutput, calls=%fused_computation.28 | convolution fusion | flops 4083941376 | bytes 9888256 | tf_op jit(solution)/shard_map/kod,fdp->fkop/dot_general | solution.py:33
  60.1 37.1 %while.10 = (s32[]{:T(128)}, bf16[2,8,72,512]{3,2,1,0:T(8,128)(2,1)}, pred[1,1152]{1,0:T(4,128)(4,1)S(1)}, s32[2]{0:T(128)S(1)}, bf16[1,8,72,1024]{3,2,1,0:T(8,1...) while((s32[]{:T(128)}, ...), condition=%wide.region_5.6_spmd, body=%wide.region_2.5_spmd.sunk | while | flops 2081200384 | bytes 5788856 | solution.py:97
  62.0 7.0 %exponential_reduce_fusion.2 = f32[8,512]{1,0:T(8,128)S(1)} fusion(pred[1152]{0:T(1024)(128)(4,1)S(1)} %reduce.5, bf16[1,8,72,1152]{3,2,1,0:T(8,128)(2,1)S(1)} %get-tuple-element.139, bf16[1,8,72,1024]{3,2,1,0:T(8,128)(2,1)} %get-tuple-element.138, s32[]{:T(128)S(6)} %select_n.67), kind=kOutput, calls=%fused_computation.5.clone.1 | convolution fusion | flops 698352768 | bytes 1934468 | tf_op jit(solution)/shard_map/while/body/eval_jaxpr/sub | solution.py:24
  69.0 9.8 %fusion.128 = bf16[2,8,72,512]{3,2,1,0:T(8,128)(2,1)} fusion(bf16[2,8,72,512]{3,2,1,0:T(8,128)(2,1)} %get-tuple-element.123, s32[]{:T(128)} %get-tuple-element.122, bf16[1,8,72,1152]{3,2,1,0:T(8,128)(2,1)} %get-tuple-element.140, f32[8,512]{1,0:T(8,128)S(1)} %exponential_reduce_fusion.2, pred[1152]{0:T(1024)(128)(4,1)S(1)} %reduce.5, ...), kind=kOutput, calls=%fused_computation.13.clone.1 | convolution fusion | flops 1382847616 | bytes 3851908 | tf_op jit(solution)/shard_map/while/body/eval_jaxpr/hpk,hek->hep/dot_general | solution.py:92
  80.3 7.0 %exponential_reduce_fusion.2 = f32[8,512]{1,0:T(8,128)S(1)} fusion(pred[1152]{0:T(1024)(128)(4,1)S(1)} %reduce.5, bf16[1,8,72,1152]{3,2,1,0:T(8,128)(2,1)S(1)} %get-tuple-element.139, bf16[1,8,72,1024]{3,2,1,0:T(8,128)(2,1)} %get-tuple-element.138, s32[]{:T(128)S(6)} %select_n.67), kind=kOutput, calls=%fused_computation.5.clone.1 | convolution fusion | flops 698352768 | bytes 1934468 | tf_op jit(solution)/shard_map/while/body/eval_jaxpr/sub | solution.py:24
  87.3 9.8 %fusion.128 = bf16[2,8,72,512]{3,2,1,0:T(8,128)(2,1)} fusion(bf16[2,8,72,512]{3,2,1,0:T(8,128)(2,1)} %get-tuple-element.123, s32[]{:T(128)} %get-tuple-element.122, bf16[1,8,72,1152]{3,2,1,0:T(8,128)(2,1)} %get-tuple-element.140, f32[8,512]{1,0:T(8,128)S(1)} %exponential_reduce_fusion.2, pred[1152]{0:T(1024)(128)(4,1)S(1)} %reduce.5, ...), kind=kOutput, calls=%fused_computation.13.clone.1 | convolution fusion | flops 1382847616 | bytes 3851908 | tf_op jit(solution)/shard_map/while/body/eval_jaxpr/hpk,hek->hep/dot_general | solution.py:92
  101.6 36.0 %all-gather.7.cloned.1.call-done = bf16[1,1152,1024]{2,1,0:T(8,128)(2,1)} async-done(((bf16[1,576,1024]{2,1,0:T(8,128)(2,1)}), bf16[1,1152,1024]{2,1,0:T(8,128)(2,1)}) %all-gather.7.cloned.1.call-update) | async-done | bytes 2359312 | tf_op jit(solution)/shard_map/all_gather | solution.py:100
  137.5 3.7 %fusion.69 = bf16[1,576,1024]{2,1,0:T(8,128)(2,1)S(1)} fusion(bf16[576,1152]{1,0:T(8,128)(2,1)S(1)} %copy-done, bf16[1,1152,1024]{2,1,0:T(8,128)(2,1)} %all-gather.7.cloned.1.call-done, bf16[1,1,576,1024]{3,2,1,0:T(8,128)(2,1)} %param.13), kind=kOutput, calls=%fused_computation.55 | convolution fusion | flops 1360723968 | bytes 6045696 | tf_op jit(solution)/shard_map/oc,fcp->fop/dot_general | solution.py:38
  141.2 4.1 %copy.44 = bf16[1,576,1024]{1,0,2:T(2,128)(2,1)} copy(bf16[1,576,1024]{2,1,0:T(8,128)(2,1)S(1)} %fusion.69) | data formatting | bytes 2359296 | tf_op jit(solution)/shard_map/convert_element_type | solution.py:101
  145.8 9.9 %reduce.3 = bf16[1024,576]{1,0:T(8,128)(2,1)S(1)} reduce(bf16[1024,1,576]{2,1,0:T(2,128)(2,1)} %bitcast.188, bf16[]{:T(256)} %broadcast.82), dimensions={1}, to_apply=%bitcast.164.reduce_sub_computation | reduce | bytes 2359298
  158.4 33.2 %all_to_all.36 = bf16[4,2,73728]{2,1,0:T(2,128)(2,1)S(1)} all-to-all(bf16[4,2,73728]{2,1,0:T(2,128)(2,1)} %reshape.124), channel_id=1, replica_groups=mesh['groups'=2,'seq'=4,'heads'=2,'cfg'=2] {'seq'}, dimensions={0} | all-to-all | bytes 2359296 | tf_op jit(solution)/shard_map/all_to_all | solution.py:102
  191.6 3.3 reshape.125
  198.3 34.3 %all-gather.11.cloned.1.call-done = bf16[4,1,1152,256]{3,2,0,1:T(8,128)(2,1)} async-done(((bf16[4,1,576,256]{3,2,0,1:T(8,128)(2,1)}), bf16[4,1,1152,256]{3,2,0,1:T(8,128)(2,1)}) %all-gather.11.cloned.1.call-update) | async-done | bytes 2359312 | tf_op jit(solution)/shard_map/all_gather | solution.py:106
  234.9 7.2 %multiply_convert_fusion = bf16[4,256,3,576]{1,3,2,0:T(8,128)(2,1)S(1)} fusion(f32[4,256]{1,0:T(4,128)S(1)} %add_rsqrt_fusion, bf16[3,576,1152]{2,1,0:T(8,128)(2,1)} %param.22, bf16[4,1,1152,256]{3,2,0,1:T(8,128)(2,1)S(1)} %copy-done.4, f32[1152]{0:T(1024)S(1)} %convert_element_type.109), kind=kOutput, calls=%fused_computation.29 | convolution fusion | flops 4083941376 | bytes 9888256 | tf_op jit(solution)/shard_map/kod,fdp->fkop/dot_general | solution.py:33
  246.9 4.1 %copy.60 = bf16[4,1,8,72,256]{3,0,4,2,1:T(4,128)(2,1)} copy(bf16[4,1,8,72,256]{4,3,2,1,0:T(8,128)(2,1)} %get-tuple-element.59) | data formatting | bytes 2359296
  251.0 5.8 %fusion.76 = f32[8,256,4,4]{3,2,1,0:T(4,128)} fusion(bf16[4,1,8,72,256]{3,0,4,2,1:T(4,128)(2,1)} %copy.60, bf16[4,1,8,72,256]{3,0,4,2,1:T(4,128)(2,1)S(1)} %copy.59), kind=kOutput, calls=%fused_computation.62 | convolution fusion | flops 4718592 | bytes 2490368 | tf_op jit(solution)/shard_map/fhep,ghep->hfgp/dot_general | solution.py:115
  264.3 5.8 %convert_bitcast_fusion = bf16[4,8,72,256]{2,0,3,1:T(4,128)(2,1)} fusion(bf16[8,4,4,256]{2,1,3,0:T(4,128)(2,1)} %copy.51, bf16[4,1,8,72,256]{3,0,4,2,1:T(4,128)(2,1)} %copy.58), kind=kOutput, calls=%fused_computation.67 | convolution fusion | flops 5308416 | bytes 2424832 | tf_op jit(solution)/shard_map/hfgp,ghep->fhep/dot_general | solution.py:119
  270.2 4.4 %copy.52 = bf16[4,8,72,256]{3,2,1,0:T(8,128)(2,1)} copy(bf16[4,8,72,256]{2,0,3,1:T(4,128)(2,1)} %convert_bitcast_fusion) | data formatting | bytes 2359296 | tf_op jit(solution)/shard_map/convert_element_type | solution.py:122
  275.0 27.5 %collective-permute-done = bf16[4,576,256]{2,1,0:T(8,128)(2,1)} collective-permute-done((bf16[4,576,256]{2,1,0:T(8,128)(2,1)}, bf16[4,576,256]{2,1,0:T(8,128)(2,1)}, u32[]{:S(2)}, u32[]{:S(2)}) %collective-permute-start) | collective-permute-done | bytes 1179680 | tf_op jit(solution)/shard_map/ppermute | solution.py:13
  302.5 5.7 %fusion.68 = bf16[4,576,256]{2,1,0:T(8,128)(2,1)S(1)} fusion(s32[]{:T(128)S(6)} %select_n.42, bf16[4,576,256]{2,1,0:T(8,128)(2,1)} %bitcast.198, bf16[4,576,256]{2,1,0:T(8,128)(2,1)} %collective-permute-done, bf16[576,1152]{1,0:T(8,128)(2,1)} %param.23, bf16[1,576,4,256]{3,1,2,0:T(8,128)(2,1)S(1)} %copy-done.2), kind=kOutput, calls=%fused_computation.53 | convolution fusion | flops 1370161152 | bytes 6045700 | tf_op jit(solution)/shard_map/oc,fcp->fop/dot_general | solution.py:38
  308.2 31.9 %all_to_all.37 = bf16[4,576,256]{2,1,0:T(8,128)(2,1)S(1)} all-to-all(bf16[4,576,256]{2,1,0:T(8,128)(2,1)S(1)} %fusion.68), channel_id=1, replica_groups=mesh['groups'=2,'seq'=4,'heads'=2,'cfg'=2] {'seq'}, dimensions={0} | all-to-all | bytes 2359296 | tf_op jit(solution)/shard_map/all_to_all | solution.py:125
  (56 shorter events, 38.1 us)
Async XLA Ops:
  6.5 131.0 %copy-start = (bf16[576,1152]{1,0:T(8,128)(2,1)S(1)}, bf16[576,1152]{1,0:T(8,128)(2,1)}, u32[]{:S(2)}) copy-start(bf16[576,1152]{1,0:T(8,128)(2,1)} %param.20) | copy-start | bytes 3981316
  6.5 41.1 %all-gather.9.cloned.1.call-start = ((), (), s32[]{:S(2)}) async-start(), calls=%async_computation.3 | async-start | bytes 3538944 | tf_op jit(solution)/shard_map/all_gather | solution.py:61
  7.3 130.3 %all-gather.7.cloned.1.call-start = ((), (), s32[]{:S(2)}) async-start(), calls=%async_computation.2 | async-start | bytes 3538944 | tf_op jit(solution)/shard_map/all_gather | solution.py:100
  47.7 2.4 copy-start.3
  101.3 131.2 %all-gather.11.cloned.1.call-start = ((), (), s32[]{:S(2)}) async-start(), calls=%async_computation.4 | async-start | bytes 3538944 | tf_op jit(solution)/shard_map/all_gather | solution.py:106
  196.8 1.5 copy-start.5
  232.6 2.4 copy-start.4
  259.7 2.2 copy-start.1
  270.2 32.3 %copy-start.2 = (bf16[1,576,4,256]{3,1,2,0:T(8,128)(2,1)S(1)}, bf16[1,576,4,256]{3,1,2,0:T(8,128)(2,1)}, u32[]{:S(2)}) copy-start(bf16[1,576,4,256]{3,1,2,0:T(8,128)(2,1)} %copy.46) | copy-start | bytes 3538948
  274.6 27.9 %collective-permute-start = (bf16[4,576,256]{2,1,0:T(8,128)(2,1)}, bf16[4,576,256]{2,1,0:T(8,128)(2,1)}, u32[]{:S(2)}, u32[]{:S(2)}) collective-permute-start(bf16[4,576,256]{2,1,0:T(8,128)(2,1)} %bitcast.197), channel_id=1, source_target_pairs={{0,2},{2,0},{1,3},{3,1},{4,6},{6,4},{5,7},{7,5},{8,10},{10,8},{9,1... | collective-permute-start | bytes 3538952 | tf_op jit(solution)/shard_map/ppermute | solution.py:13
  340.3 3.0 collective-permute-start.1
Sparse Core Ops, SparseCore 0:
  8.9 38.7 all-gather.8
  101.4 36.0 all-gather.6
  198.4 34.1 all-gather.10
